TPU v7x, 8 devices: a whole 2x2x1 slice. The times are simulated.
8 devices in a mesh: data: 2 (over z, y), stage: 4 (over x, core).
Axes of the slice: x: 2, y: 2, z: 1, core: 2. Of those that a mesh axis runs over, the one named last changes fastest.
Arguments:
- x_enc: bfloat16 [256, 128, 1024], P(('data', 'stage')), parts along dimension 0
- enc_len: int32 [256], P(('data', 'stage')), parts along dimension 0
- y: bfloat16 [256, 48, 1024], P(('data', 'stage')), parts along dimension 0
- enc_wqkv: bfloat16 [2, 1024, 3, 16, 128], replicated
- enc_wo: bfloat16 [2, 16, 128, 1024], replicated
- enc_w1: bfloat16 [2, 1024, 3072], replicated
- enc_w2: bfloat16 [2, 3072, 1024], replicated
- dec_wqkv: bfloat16 [2, 1024, 3, 16, 128], replicated
- dec_wo: bfloat16 [2, 16, 128, 1024], replicated
- cross_wq: bfloat16 [2, 1024, 8, 2, 128], replicated
- cross_wkv: bfloat16 [2, 1024, 2, 8, 128], replicated
- cross_wo: bfloat16 [2, 8, 2, 128, 1024], replicated
- dec_w1: bfloat16 [2, 1024, 3072], replicated
- dec_w2: bfloat16 [2, 3072, 1024], replicated
Outputs:
- output: bfloat16 [256, 48, 1024], P(('data', 'stage')), parts along dimension 0
There are 2 independent parts. A program takes and returns all parts, laid end to end along the dimension named above; an argument that names none is the same for every part.
All inputs are finite; a program needn't handle non-finite values.
Results may differ from a plain program's by a relative error of at most 0.0125606.
Values are sent between devices in bfloat16 or wider.
A program may use at most 1 GiB of HBM per device.

v0:
```python
import jax
import jax.numpy as jnp
from jax import lax
from jax.sharding import PartitionSpec as P, NamedSharding


def rms_norm(inputs):
    wide = inputs.astype(jnp.float32)
    return (wide * lax.rsqrt(jnp.mean(wide * wide, axis=-1, keepdims=True) + 1e-6)).astype(jnp.bfloat16)


def attend(query, keys, values, valid):
    scale = query.shape[-1] ** -0.5
    scores = jnp.einsum("bqgrd,bkgd->bgrqk", query, keys, preferred_element_type=jnp.float32) * scale
    attn_probs = jax.nn.softmax(jnp.where(valid, scores, -1e30), axis=-1).astype(jnp.bfloat16)
    return jnp.einsum("bgrqk,bkgd->bqgrd", attn_probs, values, preferred_element_type=jnp.float32).astype(jnp.bfloat16)


def self_block(state, w_qkv, w_out, valid):
    proj_qkv = jnp.einsum("bsd,dthe->tbshe", rms_norm(state), w_qkv, preferred_element_type=jnp.float32).astype(jnp.bfloat16)
    mixed = attend(proj_qkv[0][:, :, :, None, :], proj_qkv[1], proj_qkv[2], valid)
    update = jnp.einsum("bshre,hev->bsv", mixed, w_out, preferred_element_type=jnp.float32)
    return (state.astype(jnp.float32) + update).astype(jnp.bfloat16)


def ffn_block(state, w_in, w_out):
    hidden = jax.nn.gelu(jnp.einsum("bsd,df->bsf", rms_norm(state), w_in, preferred_element_type=jnp.float32)).astype(jnp.bfloat16)
    update = jnp.einsum("bsf,fd->bsd", hidden, w_out, preferred_element_type=jnp.float32)
    return (state.astype(jnp.float32) + update).astype(jnp.bfloat16)


def encoder(x_enc, enc_len, enc_wqkv, enc_wo, enc_w1, enc_w2):
    valid = (jnp.arange(x_enc.shape[1])[None, :] < enc_len[:, None])[:, None, None, None, :]
    state = x_enc
    for layer in range(enc_wqkv.shape[0]):
        state = self_block(state, enc_wqkv[layer], enc_wo[layer], valid)
        state = ffn_block(state, enc_w1[layer], enc_w2[layer])
    return rms_norm(state)


def decoder(y, kv_all, kv_len, dec_wqkv, dec_wo, cross_wq, cross_wo, dec_w1, dec_w2):
    positions = jnp.arange(y.shape[1])
    causal = positions[None, :] <= positions[:, None]
    keep = (jnp.arange(kv_all.shape[3])[None, :] < kv_len[:, None])[:, None, None, None, :]
    state = y
    for layer in range(dec_wqkv.shape[0]):
        state = self_block(state, dec_wqkv[layer], dec_wo[layer], causal)
        query = jnp.einsum("bsd,dgre->bsgre", rms_norm(state), cross_wq[layer], preferred_element_type=jnp.float32).astype(jnp.bfloat16)
        mixed = attend(query, kv_all[layer, 0], kv_all[layer, 1], keep)
        update = jnp.einsum("bsgre,grev->bsv", mixed, cross_wo[layer], preferred_element_type=jnp.float32)
        state = (state.astype(jnp.float32) + update).astype(jnp.bfloat16)
        state = ffn_block(state, dec_w1[layer], dec_w2[layer])
    return state


def solution(mesh):
    stages = mesh.shape["stage"]
    swap = [(source, (source + stages // 2) % stages) for source in range(stages)]
    rows = P(("data", "stage"))
    whole = P()

    def body(x_enc, enc_len, y, enc_wqkv, enc_wo, enc_w1, enc_w2, dec_wqkv, dec_wo, cross_wq, cross_wkv, cross_wo, dec_w1, dec_w2):
        enc_out = encoder(x_enc, enc_len, enc_wqkv, enc_wo, enc_w1, enc_w2)
        kv_all = jnp.einsum("bsd,ldtge->ltbsge", enc_out, cross_wkv, preferred_element_type=jnp.float32).astype(jnp.bfloat16)
        kv_recv = lax.ppermute(kv_all, "stage", swap)
        len_recv = lax.ppermute(enc_len, "stage", swap)
        return decoder(y, kv_recv, len_recv, dec_wqkv, dec_wo, cross_wq, cross_wo, dec_w1, dec_w2)

    return jax.shard_map(body, mesh=mesh, in_specs=(rows, rows, rows) + (whole,) * 11, out_specs=rows, check_vma=False)
```

profile of v0, /device:TPU:0, one launch (start us, length us, event | category | flops | bytes accessed | tf_op | source)
XLA Modules:
  0.0 1557.4 jit_solution(12302234560106516640)
XLA Ops:
  0.7 19.0 %fusion.374 = (bf16[1,1024,3,16,128]{4,3,2,1,0:T(8,128)(2,1)}, bf16[1,1024,3,16,128]{4,3,2,1,0:T(8,128)(2,1)}) fusion(bf16[2,1024,3,16,128]{4,3,2,1,0:T(8,128)(2,1)} %param.17), kind=kLoop, calls=%fused_computation.328 | loop fusion | bytes 50331648 | tf_op jit(solution)/shard_map/slice | solution.py:36
  21.5 62.4 %convert_bitcast_fusion.1 = bf16[3,32,128,16,128]{4,2,3,0,1:T(8,128)(2,1)} fusion(bf16[1,1024,3,16,128]{4,3,2,1,0:T(8,128)(2,1)} %get-tuple-element.8, bf16[32,128,1024]{2,1,0:T(8,128)(2,1)} %param.14, f32[32,128]{1,0:T(8,128)S(1)} %add_rsqrt_fusion.9), kind=kOutput, calls=%fused_computation.21 | convolution fusion | flops 51577356288 | bytes 71319552 | tf_op jit(solution)/shard_map/bsd,dthe->tbshe/dot_general | solution.py:20
  83.9 25.7 %bitcast_reduce_fusion.1 = (f32[32,16,128]{2,1,0:T(8,128)S(1)}, f32[32,16,128,128]{3,2,1,0:T(8,128)}) fusion(pred[32,128]{1,0:T(8,128)(4,1)S(1)} %iota_compare_fusion.2, bf16[3,32,128,16,128]{4,2,3,0,1:T(8,128)(2,1)} %convert_bitcast_fusion.1), kind=kOutput, calls=%fused_computation.27 | convolution fusion | flops 2172583936 | bytes 67375104 | tf_op jit(solution)/shard_map/bqgrd,bkgd->bgrqk/dot_general | solution.py:14
  124.4 23.7 %fusion.118.clone.5 = bf16[32,128,16,128]{1,3,2,0:T(8,128)(2,1)} fusion(f32[32,16,128]{2,1,0:T(8,128)S(1)} %fusion.20, f32[32,16,128,128]{3,2,1,0:T(8,128)} %get-tuple-element.14, f32[32,16,128]{2,1,0:T(8,128)S(1)} %get-tuple-element.13, pred[32,128]{1,0:T(8,128)(4,1)S(1)} %iota_compare_fusion.2, ...), kind=kOutput, calls=%fused_computation.96.clone.clone.clone.clone.clone.2 | convolution fusion | flops 2197815296 | bytes 67637248 | tf_op jit(solution)/shard_map/bgrqk,bkgd->bqgrd/dot_general | solution.py:16
  148.2 26.9 %fusion.43 = (f32[32,128]{1,0:T(8,128)S(1)}, bf16[32,128,1024]{2,1,0:T(8,128)(2,1)}) fusion(bf16[2,16,128,1024]{3,2,1,0:T(8,128)(2,1)} %param.18, bf16[32,128,1024]{2,1,0:T(8,128)(2,1)} %param.14, bf16[32,128,16,128]{1,3,2,0:T(8,128)(2,1)} %fusion.118.clone.5), kind=kOutput, calls=%fused_computation.74 | convolution fusion | flops 17205030912 | bytes 37765120 | tf_op jit(solution)/shard_map/bshre,hev->bsv/dot_general | solution.py:22
  175.1 40.7 %fusion.9.clone.1.clone.5 = bf16[32,128,3072]{2,1,0:T(8,128)(2,1)} fusion(bf16[32,128,1024]{2,1,0:T(8,128)(2,1)} %get-tuple-element.16, f32[32,128]{1,0:T(8,128)S(1)} %add_rsqrt_fusion.8, bf16[2,1024,3072]{2,1,0:T(8,128)(2,1)} %param.19), kind=kOutput, calls=%fused_computation.11.clone.clone.clone.clone.clone.2 | convolution fusion | flops 25895632896 | bytes 39862272 | tf_op jit(solution)/shard_map/bsd,df->bsf/dot_general | solution.py:27
  215.9 33.6 %fusion.46 = (f32[32,128]{1,0:T(8,128)S(1)}, bf16[32,128,1024]{2,1,0:T(8,128)(2,1)}) fusion(bf16[2,3072,1024]{2,1,0:T(8,128)(2,1)} %param.20, bf16[32,128,1024]{2,1,0:T(8,128)(2,1)S(1)} %copy-done.10, bf16[32,128,3072]{2,1,0:T(8,128)(2,1)} %fusion.9.clone.1.clone.5), kind=kOutput, calls=%fused_computation.77 | convolution fusion | flops 25794965504 | bytes 48250880 | tf_op jit(solution)/shard_map/bsf,fd->bsd/dot_general | solution.py:28
  249.6 62.4 %convert_bitcast_fusion = bf16[3,32,128,16,128]{4,2,3,0,1:T(8,128)(2,1)} fusion(bf16[1,1024,3,16,128]{4,3,2,1,0:T(8,128)(2,1)} %get-tuple-element.7, bf16[32,128,1024]{2,1,0:T(8,128)(2,1)} %get-tuple-element.18, f32[32,128]{1,0:T(8,128)S(1)} %add_rsqrt_fusion.7), kind=kOutput, calls=%fused_computation.20 | convolution fusion | flops 51577356288 | bytes 71319552 | tf_op jit(solution)/shard_map/bsd,dthe->tbshe/dot_general | solution.py:20
  312.0 25.2 %bitcast_reduce_fusion = (f32[32,16,128]{2,1,0:T(8,128)S(1)}, f32[32,16,128,128]{3,2,1,0:T(8,128)}) fusion(pred[32,128]{1,0:T(8,128)(4,1)S(1)} %copy-done.5, bf16[3,32,128,16,128]{4,2,3,0,1:T(8,128)(2,1)} %convert_bitcast_fusion), kind=kOutput, calls=%fused_computation.23 | convolution fusion | flops 2172583936 | bytes 67375104 | tf_op jit(solution)/shard_map/bqgrd,bkgd->bgrqk/dot_general | solution.py:14
  352.2 23.7 %fusion.122.clone.5 = bf16[32,128,16,128]{1,3,2,0:T(8,128)(2,1)} fusion(f32[32,16,128]{2,1,0:T(8,128)S(1)} %fusion.21, f32[32,16,128,128]{3,2,1,0:T(8,128)} %get-tuple-element.20, f32[32,16,128]{2,1,0:T(8,128)S(1)} %get-tuple-element.19, pred[32,128]{1,0:T(8,128)(4,1)S(1)} %copy-done.5, ...), kind=kOutput, calls=%fused_computation.94.clone.clone.clone.clone.clone.2 | convolution fusion | flops 2197815296 | bytes 67637248 | tf_op jit(solution)/shard_map/bgrqk,bkgd->bqgrd/dot_general | solution.py:16
  375.9 26.9 %fusion.49 = (f32[32,128]{1,0:T(8,128)S(1)}, bf16[32,128,1024]{2,1,0:T(8,128)(2,1)}) fusion(bf16[2,16,128,1024]{3,2,1,0:T(8,128)(2,1)} %param.18, bf16[32,128,1024]{2,1,0:T(8,128)(2,1)} %get-tuple-element.18, bf16[32,128,16,128]{1,3,2,0:T(8,128)(2,1)} %fusion.122.clone.5), kind=kOutput, calls=%fused_computation.80 | convolution fusion | flops 17205030912 | bytes 37765120 | tf_op jit(solution)/shard_map/bshre,hev->bsv/dot_general | solution.py:22
  402.8 40.7 %fusion.17.clone.1.clone.5 = bf16[32,128,3072]{2,1,0:T(8,128)(2,1)} fusion(bf16[32,128,1024]{2,1,0:T(8,128)(2,1)} %get-tuple-element.22, f32[32,128]{1,0:T(8,128)S(1)} %add_rsqrt_fusion.6, bf16[2,1024,3072]{2,1,0:T(8,128)(2,1)} %param.19), kind=kOutput, calls=%fused_computation.19.clone.clone.clone.clone.clone.2 | convolution fusion | flops 25895632896 | bytes 39862272 | tf_op jit(solution)/shard_map/bsd,df->bsf/dot_general | solution.py:27
  443.5 33.6 %fusion.38 = (f32[32,128]{1,0:T(8,128)S(1)}, bf16[32,128,1024]{2,1,0:T(8,128)(2,1)}) fusion(bf16[2,3072,1024]{2,1,0:T(8,128)(2,1)} %param.20, bf16[32,128,1024]{2,1,0:T(8,128)(2,1)S(1)} %copy-done.9, bf16[32,128,3072]{2,1,0:T(8,128)(2,1)} %fusion.17.clone.1.clone.5), kind=kOutput, calls=%fused_computation.69 | convolution fusion | flops 25794965504 | bytes 48250880 | tf_op jit(solution)/shard_map/bsf,fd->bsd/dot_general | solution.py:28
  477.2 43.1 %convert_bitcast_fusion.2 = bf16[2,2,32,128,8,128]{5,3,4,1,0,2:T(8,128)(2,1)} fusion(bf16[32,128,1024]{2,1,0:T(8,128)(2,1)} %get-tuple-element.24, bf16[2,1024,2,8,128]{4,3,2,1,0:T(8,128)(2,1)} %param.24, f32[32,128]{1,0:T(8,128)S(1)} %add_rsqrt_fusion.5), kind=kOutput, calls=%fused_computation.30 | convolution fusion | flops 34389098496 | bytes 50348032 | tf_op jit(solution)/shard_map/bsd,ldtge->ltbsge/dot_general | solution.py:64
  524.4 18.6 %fusion.373 = (bf16[1,1024,3,16,128]{4,3,2,1,0:T(8,128)(2,1)}, bf16[1,1024,3,16,128]{4,3,2,1,0:T(8,128)(2,1)}) fusion(bf16[2,1024,3,16,128]{4,3,2,1,0:T(8,128)(2,1)} %param.21), kind=kLoop, calls=%fused_computation.327 | loop fusion | bytes 50331648 | tf_op jit(solution)/shard_map/slice | solution.py:47
  543.1 28.3 %convert_bitcast_fusion.4 = bf16[3,32,48,16,128]{4,2,3,0,1:T(8,128)(2,1)} fusion(bf16[1,1024,3,16,128]{4,3,2,1,0:T(8,128)(2,1)} %get-tuple-element.6, bf16[32,48,1024]{2,1,0:T(8,128)(2,1)S(1)} %copy-done.1, f32[32,48]{1,0:T(8,128)S(1)} %add_rsqrt_fusion.10), kind=kOutput, calls=%fused_computation.68 | convolution fusion | flops 19341508608 | bytes 34609152 | tf_op jit(solution)/shard_map/bsd,dthe->tbshe/dot_general | solution.py:20
  618.7 624.7 %collective-permute-done.1 = s32[32]{0:T(128)S(1)} collective-permute-done((s32[32]{0:T(128)S(1)}, s32[32]{0:T(128)S(1)}, u32[]{:S(2)}, u32[]{:S(2)}) %collective-permute-start.1) | collective-permute-done | bytes 160 | tf_op jit(solution)/shard_map/ppermute | solution.py:66
  1243.5 19.2 %fusion.106 = f32[32,8,128,48,2]{2,3,4,1,0:T(8,128)} fusion(bf16[2,2,32,128,8,128]{5,3,4,1,0,2:T(8,128)(2,1)} %collective-permute-done, bf16[1024,8,2,128,1]{3,2,1,0,4:T(2,128)(2,1)} %get-tuple-element.10, bf16[32,48,1024]{2,1,0:T(8,128)(2,1)} %get-tuple-element.26, f32[32,48]{1,0:T(8,128)S(1)} %add_rsqrt_fusion.4), kind=kOutput, calls=%fused_computation.163 | convolution fusion | flops 7255621632 | bytes 28317696 | tf_op jit(solution)/shard_map/bqgrd,bkgd->bgrqk/dot_general | solution.py:14
  1277.9 50.4 %fusion.292.clone.5 = bf16[32,48,8,2,128]{4,1,3,2,0:T(8,128)(2,1)} fusion(f32[32,8,2,48]{3,2,1,0:T(2,128)S(1)} %fusion.389, bf16[2,2,32,128,8,128]{5,3,4,1,0,2:T(8,128)(2,1)} %collective-permute-done, f32[32,8,128,48,2]{2,3,4,1,0:T(8,128)} %fusion.106, pred[32,128]{1,0:T(8,128)(4,1)S(1)} %iota_compare_fusion.1), kind=kOutput, calls=%fused_computation.215.clone.clone.clone.clone.clone.2 | convolution fusion | flops 830496896 | bytes 40116224 | tf_op jit(solution)/shard_map/bgrqk,bkgd->bqgrd/dot_general | solution.py:16
  1339.7 27.2 %fusion.132 = (f32[32,48]{1,0:T(8,128)S(1)}, bf16[32,48,1024]{2,1,0:T(8,128)(2,1)}) fusion(bf16[2,3072,1024]{2,1,0:T(8,128)(2,1)} %param.27, bf16[2,1024,3072]{2,1,0:T(8,128)(2,1)} %param.26, bf16[32,48,1024]{2,1,0:T(8,128)(2,1)} %get-tuple-element.28, f32[32,48]{1,0:T(8,128)S(1)} %add_rsqrt_fusion.3), kind=kOutput, calls=%fused_computation.182 | convolution fusion | flops 19383973888 | bytes 22032384 | tf_op jit(solution)/shard_map/bsf,fd->bsd/dot_general | solution.py:28
  1366.9 28.3 %convert_bitcast_fusion.3 = bf16[3,32,48,16,128]{4,2,3,0,1:T(8,128)(2,1)} fusion(bf16[1,1024,3,16,128]{4,3,2,1,0:T(8,128)(2,1)} %get-tuple-element.5, bf16[32,48,1024]{2,1,0:T(8,128)(2,1)} %get-tuple-element.30, f32[32,48]{1,0:T(8,128)S(1)} %add_rsqrt_fusion.2), kind=kOutput, calls=%fused_computation.67 | convolution fusion | flops 19341508608 | bytes 34609152 | tf_op jit(solution)/shard_map/bsd,dthe->tbshe/dot_general | solution.py:20
  1433.7 19.6 %fusion.104 = f32[32,8,128,48,2]{2,3,4,1,0:T(8,128)} fusion(bf16[2,2,32,128,8,128]{5,3,4,1,0,2:T(8,128)(2,1)} %collective-permute-done, bf16[1024,8,2,128,1]{3,2,1,0,4:T(2,128)(2,1)} %get-tuple-element.9, bf16[32,48,1024]{2,1,0:T(8,128)(2,1)} %get-tuple-element.34, f32[32,48]{1,0:T(8,128)S(1)} %add_rsqrt_fusion.1), kind=kOutput, calls=%fused_computation.159 | convolution fusion | flops 7255621632 | bytes 28317696 | tf_op jit(solution)/shard_map/bqgrd,bkgd->bgrqk/dot_general | solution.py:14
  1468.1 50.6 %fusion.296.clone.5 = bf16[32,48,8,2,128]{4,1,3,2,0:T(8,128)(2,1)} fusion(f32[32,8,2,48]{3,2,1,0:T(2,128)S(1)} %fusion.398, bf16[2,2,32,128,8,128]{5,3,4,1,0,2:T(8,128)(2,1)} %collective-permute-done, f32[32,8,128,48,2]{2,3,4,1,0:T(8,128)} %fusion.104, pred[32,128]{1,0:T(8,128)(4,1)S(1)} %copy-done.7), kind=kOutput, calls=%fused_computation.209.clone.clone.clone.clone.clone.2 | convolution fusion | flops 830496896 | bytes 40116224 | tf_op jit(solution)/shard_map/bgrqk,bkgd->bqgrd/dot_general | solution.py:16
  1530.1 27.1 %fusion.140 = bf16[32,48,1024]{2,1,0:T(8,128)(2,1)} fusion(bf16[32,48,1024]{2,1,0:T(8,128)(2,1)} %get-tuple-element.36, bf16[2,3072,1024]{2,1,0:T(8,128)(2,1)} %param.27, bf16[2,1024,3072]{2,1,0:T(8,128)(2,1)} %param.26, f32[32,48]{1,0:T(8,128)S(1)} %add_rsqrt_fusion), kind=kOutput, calls=%fused_computation.190 | convolution fusion | flops 19379257344 | bytes 22026240 | tf_op jit(solution)/shard_map/bsf,fd->bsd/dot_general | solution.py:28
  (58 shorter events, 175.2 us)
Async XLA Ops:
  0.7 123.7 %copy-start.4 = (pred[32,128]{1,0:T(8,128)(4,1)}, pred[32,128]{1,0:T(8,128)(4,1)S(1)}, u32[]{:S(2)}) copy-start(pred[32,128]{1,0:T(8,128)(4,1)S(1)} %iota_compare_fusion.2) | copy-start | bytes 12292
  0.7 19.0 %copy-start = (bf16[32,128,1024]{2,1,0:T(8,128)(2,1)S(1)}, bf16[32,128,1024]{2,1,0:T(8,128)(2,1)}, u32[]{:S(2)}) copy-start(bf16[32,128,1024]{2,1,0:T(8,128)(2,1)} %param.14) | copy-start | bytes 25165828
  175.1 40.7 %copy-start.10 = (bf16[32,128,1024]{2,1,0:T(8,128)(2,1)S(1)}, bf16[32,128,1024]{2,1,0:T(8,128)(2,1)}, u32[]{:S(2)}) copy-start(bf16[32,128,1024]{2,1,0:T(8,128)(2,1)} %get-tuple-element.16) | copy-start | bytes 25165828
  249.5 62.4 %copy-start.5 = (pred[32,128]{1,0:T(8,128)(4,1)S(1)}, pred[32,128]{1,0:T(8,128)(4,1)}, u32[]{:S(2)}) copy-start(pred[32,128]{1,0:T(8,128)(4,1)} %copy-done.4) | copy-start | bytes 12292
  402.8 40.7 %copy-start.9 = (bf16[32,128,1024]{2,1,0:T(8,128)(2,1)S(1)}, bf16[32,128,1024]{2,1,0:T(8,128)(2,1)}, u32[]{:S(2)}) copy-start(bf16[32,128,1024]{2,1,0:T(8,128)(2,1)} %get-tuple-element.22) | copy-start | bytes 25165828
  477.2 46.5 %copy-start.8 = (s32[32]{0:T(128)S(1)}, s32[32]{0:T(128)}, u32[]{:S(2)}) copy-start(s32[32]{0:T(128)} %param.15) | copy-start | bytes 388
  477.2 46.5 %copy-start.1 = (bf16[32,48,1024]{2,1,0:T(8,128)(2,1)S(1)}, bf16[32,48,1024]{2,1,0:T(8,128)(2,1)}, u32[]{:S(2)}) copy-start(bf16[32,48,1024]{2,1,0:T(8,128)(2,1)} %param.16) | copy-start | bytes 9437188
  520.3 723.2 %collective-permute-start = (bf16[2,2,32,128,8,128]{5,3,4,1,0,2:T(8,128)(2,1)}, bf16[2,2,32,128,8,128]{5,3,4,1,0,2:T(8,128)(2,1)}, u32[]{:S(2)}, u32[]{:S(2)}) collective-permute-start(bf16[2,2,32,128,8,128]{5,3,4,1,0,2:T(8,128)(2,1)} %convert_bitcast_fusion.2), channel_id=1, source_target_pairs={{0,2},{1,3},{2,0},{3,1},{4,6},{5,7},{6,4},{7,5}} | collective-permute-start | bytes 100663304 | tf_op jit(solution)/shard_map/ppermute | solution.py:65
  523.7 719.8 %collective-permute-start.1 = (s32[32]{0:T(128)S(1)}, s32[32]{0:T(128)S(1)}, u32[]{:S(2)}, u32[]{:S(2)}) collective-permute-start(s32[32]{0:T(128)S(1)} %copy-done.8), channel_id=1, source_target_pairs={{0,2},{1,3},{2,0},{3,1},{4,6},{5,7},{6,4},{7,5}} | collective-permute-start | bytes 392 | tf_op jit(solution)/shard_map/ppermute | solution.py:66
  523.7 77.9 %copy-start.2 = (pred[48,48]{0,1:T(8,128)(4,1)}, pred[48,48]{0,1:T(8,128)(4,1)S(1)}, u32[]{:S(2)}) copy-start(pred[48,48]{0,1:T(8,128)(4,1)S(1)} %iota_compare_fusion) | copy-start | bytes 6916
  1243.5 34.4 %copy-start.6 = (pred[32,128]{1,0:T(8,128)(4,1)}, pred[32,128]{1,0:T(8,128)(4,1)S(1)}, u32[]{:S(2)}) copy-start(pred[32,128]{1,0:T(8,128)(4,1)S(1)} %iota_compare_fusion.1) | copy-start | bytes 12292
  1277.9 50.4 %copy-start.11 = (bf16[32,48,1024]{2,1,0:T(8,128)(2,1)S(1)}, bf16[32,48,1024]{2,1,0:T(8,128)(2,1)}, u32[]{:S(2)}) copy-start(bf16[32,48,1024]{2,1,0:T(8,128)(2,1)} %get-tuple-element.26) | copy-start | bytes 9437188
  1366.9 28.4 %copy-start.3 = (pred[48,48]{0,1:T(8,128)(4,1)S(1)}, pred[48,48]{0,1:T(8,128)(4,1)}, u32[]{:S(2)}) copy-start(pred[48,48]{0,1:T(8,128)(4,1)} %copy-done.2) | copy-start | bytes 6916
  1433.7 19.6 %copy-start.7 = (pred[32,128]{1,0:T(8,128)(4,1)S(1)}, pred[32,128]{1,0:T(8,128)(4,1)}, u32[]{:S(2)}) copy-start(pred[32,128]{1,0:T(8,128)(4,1)} %copy-done.6) | copy-start | bytes 12292
  1468.1 50.6 %copy-start.12 = (bf16[32,48,1024]{2,1,0:T(8,128)(2,1)S(1)}, bf16[32,48,1024]{2,1,0:T(8,128)(2,1)}, u32[]{:S(2)}) copy-start(bf16[32,48,1024]{2,1,0:T(8,128)(2,1)} %get-tuple-element.34) | copy-start | bytes 9437188
where the time goes:
time: 1570 us; the launch traced here: 1560 us
  matrix products  802 us (51%)
  waiting for transfers between devices  625 us (40%)
  other arithmetic  80.9 us (5%)
  local copies, waits for them, and re-layouts  46.1 us (3%)
    ppermute x1, waiting for transfers between devices, body(): len_recv = lax.ppermute(enc_len, 'stage', swap)  625 us
    dot_general x4, matrix products, self_block(): jnp.einsum('bsd,dthe->tbshe', rms_norm(state), w_qkv, preferred_element_t...  181 us
    dot_general x4, matrix products, attend(): jnp.einsum('bgrqk,bkgd->bqgrd', attn_probs, values, preferred_element_typ...  148 us
    dot_general x4, matrix products, ffn_block(): jnp.einsum('bsf,fd->bsd', hidden, w_out, preferred_element_type=jnp.float32)  121 us
    dot_general x6, matrix products, attend(): jnp.einsum('bqgrd,bkgd->bgrqk', query, keys, preferred_element_type=jnp.f...  115 us
    dot_general x4, matrix products, self_block(): jnp.einsum('bshre,hev->bsv', mixed, w_out, preferred_element_type=jnp.flo...  88.1 us
    dot_general x2, matrix products, ffn_block(): jnp.einsum('bsd,df->bsf', rms_norm(state), w_in, preferred_element_type=j...  81.5 us
    reduce_sum x4, other arithmetic, attend(): jax.nn.softmax(jnp.where(valid, scores, -1e+30), axis=-1)  47.5 us
  transfers between devices with their start and end apart: 2, of which 1 were waited for; matrix products, arithmetic and copies ran while one was open for 6% of the time, Pallas kernels for 0%

commit v1 on v0

v1 whole, which is shorter than its diff:
```python
import jax
import jax.numpy as jnp
from jax import lax
from jax.experimental import pallas as pl
from jax.experimental.pallas import tpu as pltpu
from jax.sharding import PartitionSpec as P

BF = jnp.bfloat16
F32 = jnp.float32
D = 1024
HEADS = 16
HD = 128
FF = 3072
S_ENC = 128
S_DEC = 48
TILE = 256
DTILE = 192
GROUP = 4
LOG2E = 1.4426950408889634
SCALE2 = HD ** -0.5 * LOG2E
VMEM_LIMIT = 66_000_000


def rms(h):
    wide = h.astype(F32)
    return (wide * lax.rsqrt(jnp.mean(wide * wide, axis=-1, keepdims=True) + 1e-6)).astype(BF)


def mm(lhs, rhs):
    return jnp.dot(lhs, rhs, preferred_element_type=F32)


def gelu(v):
    return jax.nn.gelu(v, approximate=True)


def softmax(s):
    m = jnp.max(s, axis=-1, keepdims=True)
    e = jnp.exp2((s - m) * SCALE2)
    return (e * (1.0 / jnp.sum(e, axis=-1, keepdims=True))).astype(BF)


def qk(q, k):
    return lax.dot_general(q, k, (((1,), (1,)), ((), ())), preferred_element_type=F32)


def prefix_starts(len_ref, starts, n):
    def step(i, pos):
        starts[i] = pos
        return pos + ((len_ref[i] + 15) // 16) * 16
    return lax.fori_loop(0, n, step, jnp.int32(0))


def head_copies(hbm, buf, sem, layer, heads, first):
    return [pltpu.make_async_copy(hbm.at[layer, c], buf.at[:, c * HD:(c + 1) * HD], sem.at[first + c]) for c in heads]


def start_all(copies):
    for c in copies:
        c.start()


def wait_all(copies):
    for c in copies:
        c.wait()


def enc_kernel(n_seq, len_ref, x_hbm, wqkv_hbm, wo_hbm, w1_hbm, w2_hbm, out_hbm,
               starts, h, qkv_a, qkv_b, o, s_scr, p_scr, xn, hid, wqkv, wo, w1, w2, sem_x, sem_w, sem_o):
    gw = GROUP * HD
    n_groups = HEADS // GROUP
    n_pair = n_seq // 2
    bufs = (qkv_a, qkv_b)

    def qkv_copies(layer, g):
        heads = [t * HEADS + g * GROUP + c for t in range(3) for c in range(GROUP)]
        return head_copies(wqkv_hbm, wqkv, sem_w, layer, heads, 0)

    def wo_copy(layer):
        return pltpu.make_async_copy(wo_hbm.at[layer], wo, sem_w.at[48])

    def w1_copy(layer):
        return pltpu.make_async_copy(w1_hbm.at[layer], w1, sem_w.at[49])

    def w2_copy(layer):
        return pltpu.make_async_copy(w2_hbm.at[layer], w2, sem_w.at[50])

    total = prefix_starts(len_ref, starts, n_seq)
    nt = (total + TILE - 1) // TILE
    end = pl.multiple_of(nt * TILE, TILE)
    last = pl.multiple_of((nt - 1) * TILE, TILE)
    h[pl.ds(last, TILE), :] = jnp.zeros((TILE, D), BF)

    def x_copy(s, j):
        src = x_hbm.at[pl.ds(pl.multiple_of(s * S_ENC + j * 16, 16), 16), :]
        dst = h.at[pl.ds(pl.multiple_of(starts[s] + j * 16, 16), 16), :]
        return pltpu.make_async_copy(src, dst, sem_x)

    def each_piece(fn):
        def seq(s, c):
            lax.fori_loop(0, (len_ref[s] + 15) // 16, lambda j, d: (fn(s, j), d)[1], 0)
            return c
        lax.fori_loop(0, n_seq, seq, 0)

    each_piece(lambda s, j: x_copy(s, j).start())
    for g in range(n_groups):
        start_all(qkv_copies(0, g))
    wo_copy(0).start()
    w1_copy(0).start()
    w2_copy(0).start()
    o[pl.ds(last, TILE), :] = jnp.zeros((TILE, HEADS * HD), BF)
    for buf in bufs:
        buf[pl.ds(end, S_ENC), :] = jnp.zeros((S_ENC, 3 * gw), BF)
    each_piece(lambda s, j: x_copy(s, j).wait())

    def layer_step(layer, carry):
        def project_part(i, g, t):
            r = pl.ds(pl.multiple_of(i * TILE, TILE), TILE)
            c0 = (t * HEADS + g * GROUP) * HD
            bufs[g % 2][r, t * gw:(t + 1) * gw] = mm(xn[...], wqkv[:, c0:c0 + gw]).astype(BF)

        def norm(i):
            xn[...] = rms(h[pl.ds(pl.multiple_of(i * TILE, TILE), TILE), :])

        def rows_of(s):
            return pl.ds(pl.multiple_of(starts[s], 16), S_ENC)

        def scores(pi, g):
            buf = bufs[g % 2]
            for b in range(2):
                s = 2 * pi + b
                r = rows_of(s)
                keep = lax.broadcasted_iota(jnp.int32, (S_ENC, S_ENC), 1) < len_ref[s]
                for hh in range(GROUP):
                    c = hh * HD
                    s_scr[b * GROUP + hh] = jnp.where(keep, qk(buf[r, c:c + HD], buf[r, gw + c:gw + c + HD]), -1e30)

        def probs():
            for j in range(2 * GROUP):
                p_scr[j] = softmax(s_scr[j])

        def values(pi, g):
            buf = bufs[g % 2]
            for b in range(2):
                r = rows_of(2 * pi + b)
                for hh in range(GROUP):
                    c = hh * HD
                    o[r, g * gw + c:g * gw + c + HD] = mm(p_scr[b * GROUP + hh], buf[r, 2 * gw + c:2 * gw + c + HD]).astype(BF)

        for g in range(n_groups + 1):
            if g < n_groups:
                wait_all(qkv_copies(layer, g))

            def project_only(i, c):
                norm(i)
                for t in range(3):
                    project_part(i, g, t)
                return c

            def both(i, c):
                scores(i, g - 1)
                norm(i)
                project_part(i, g, 0)
                probs()
                project_part(i, g, 1)
                project_part(i, g, 2)
                values(i, g - 1)
                return c

            def attend_only(i, c):
                scores(i, g - 1)
                probs()
                values(i, g - 1)
                return c

            if g == 0:
                lax.fori_loop(0, nt, project_only, 0)
            elif g < n_groups:
                lax.fori_loop(0, nt, both, 0)
                lax.fori_loop(nt, n_pair, attend_only, 0)
            else:
                lax.fori_loop(0, n_pair, attend_only, 0)

            if g < n_groups:
                @pl.when(layer == 0)
                def _():
                    start_all(qkv_copies(1, g))

        wo_copy(layer).wait()
        w1_copy(layer).wait()
        w2_copy(layer).wait()

        def ffn_tile(i, c):
            r = pl.ds(pl.multiple_of(i * TILE, TILE), TILE)
            for n in range(0, D, 512):
                h[r, n:n + 512] = (h[r, n:n + 512].astype(F32) + mm(o[r, :], wo[:, n:n + 512])).astype(BF)
            xn[...] = rms(h[r, :])
            for n in range(0, FF, 512):
                hid[:, n:n + 512] = gelu(mm(xn[...], w1[:, n:n + 512])).astype(BF)
            for n in range(0, D, 512):
                h[r, n:n + 512] = (h[r, n:n + 512].astype(F32) + mm(hid[...], w2[:, n:n + 512])).astype(BF)
            return c
        lax.fori_loop(0, nt, ffn_tile, 0)

        @pl.when(layer == 0)
        def _():
            wo_copy(1).start()
            w1_copy(1).start()
            w2_copy(1).start()
        return carry
    lax.fori_loop(0, 2, layer_step, 0)

    def out_copy(i):
        r = pl.ds(pl.multiple_of(i * TILE, TILE), TILE)
        return pltpu.make_async_copy(h.at[r, :], out_hbm.at[r, :], sem_o)

    def out_tile(i, c):
        r = pl.ds(pl.multiple_of(i * TILE, TILE), TILE)
        h[r, :] = rms(h[r, :])
        out_copy(i).start()
        return c
    lax.fori_loop(0, nt, out_tile, 0)
    lax.fori_loop(0, nt, lambda i, c: (out_copy(i).wait(), c)[1], 0)


ANY = pl.BlockSpec(memory_space=pl.ANY)
SMEM = pl.BlockSpec(memory_space=pltpu.SMEM)


def encode(lens, x, wqkv, wo, w1, w2):
    n_seq = lens.shape[0]
    rows = n_seq * S_ENC
    pad = rows + S_ENC
    tokens = rows * 5 // 8
    cost = pl.CostEstimate(flops=tokens * 2 * 30_400_000, bytes_accessed=70_000_000, transcendentals=0)
    return pl.pallas_call(
        lambda *refs: enc_kernel(n_seq, *refs),
        out_shape=jax.ShapeDtypeStruct((rows, D), BF),
        in_specs=[SMEM] + [ANY] * 5,
        out_specs=ANY,
        scratch_shapes=[
            pltpu.SMEM((n_seq,), jnp.int32),
            pltpu.VMEM((rows, D), BF),
            pltpu.VMEM((pad, 3 * GROUP * HD), BF),
            pltpu.VMEM((pad, 3 * GROUP * HD), BF),
            pltpu.VMEM((pad, 2 * D), BF),
            pltpu.VMEM((2 * GROUP, S_ENC, S_ENC), F32),
            pltpu.VMEM((2 * GROUP, S_ENC, S_ENC), BF),
            pltpu.VMEM((TILE, D), BF),
            pltpu.VMEM((TILE, FF), BF),
            pltpu.VMEM((D, 6 * D), BF),
            pltpu.VMEM((2 * D, D), BF),
            pltpu.VMEM((D, FF), BF),
            pltpu.VMEM((FF, D), BF),
            pltpu.SemaphoreType.DMA,
            pltpu.SemaphoreType.DMA((51,)),
            pltpu.SemaphoreType.DMA,
        ],
        compiler_params=pltpu.CompilerParams(vmem_limit_bytes=VMEM_LIMIT),
        cost_estimate=cost,
        name="encode",
    )(lens, x, wqkv, wo, w1, w2)


def dec_kernel(n_seq, len_ref, y_hbm, h1_hbm, h2_hbm, wqkv_hbm, wo_hbm, wq_hbm, wkv_hbm, woc_hbm, w1_hbm, w2_hbm, out_hbm,
               starts, z, kv, ht, qkv, o, s_scr, p_scr, xn, hid, wqkv, wo, wq, wkv, woc, w1, w2, sem_y, sem_w, sem_h):
    tokens = n_seq * S_DEC
    n_half = n_seq // 2
    wide = {0: (wqkv_hbm, wqkv, 48, 0), 2: (wkv_hbm, wkv, 16, 48), 3: (wq_hbm, wq, 16, 64)}
    flat = {1: (wo_hbm, wo, 80), 4: (woc_hbm, woc, 81), 5: (w1_hbm, w1, 82), 6: (w2_hbm, w2, 83)}

    class Copies:
        def __init__(self, copies):
            self.copies = copies

        def start(self):
            start_all(self.copies)

        def wait(self):
            wait_all(self.copies)

    def w_copy(layer, i):
        if i in wide:
            hbm, buf, n, first = wide[i]
            return Copies(head_copies(hbm, buf, sem_w, layer, range(n), first))
        hbm, buf, k = flat[i]
        return Copies([pltpu.make_async_copy(hbm.at[layer], buf, sem_w.at[k])])

    y_copy = pltpu.make_async_copy(y_hbm, z, sem_y)
    y_copy.start()
    for i in range(7):
        w_copy(0, i).start()

    def step(i, pos):
        pos = jnp.where(i == n_half, 0, pos)
        starts[i] = pos
        return pos + ((len_ref[i] + 15) // 16) * 16

    def total_of(lo):
        return lax.fori_loop(lo, lo + n_half, lambda i, t: t + ((len_ref[i] + 15) // 16) * 16, jnp.int32(0))
    lax.fori_loop(0, n_seq, step, jnp.int32(0))
    nts = [(total_of(hf * n_half) + TILE - 1) // TILE for hf in range(2)]
    y_copy.wait()

    pair = 2 * S_DEC
    qpos = lax.broadcasted_iota(jnp.int32, (pair, pair), 0)
    kpos = lax.broadcasted_iota(jnp.int32, (pair, pair), 1)
    causal = (kpos <= qpos) & ((kpos >= S_DEC) == (qpos >= S_DEC))

    def prefetch(layer, i):
        @pl.when(layer == 0)
        def _():
            w_copy(1, i).start()

    def layer_step(layer, carry):
        w_copy(layer, 0).wait()
        w_copy(layer, 1).wait()

        def self_tile(i, c):
            r = pl.ds(pl.multiple_of(i * DTILE, DTILE), DTILE)
            xn[:DTILE, :] = rms(z[r, :])
            gw = GROUP * HD
            n_groups = HEADS // GROUP
            n_pairs = DTILE // pair

            def project(g):
                for t in range(3):
                    c0 = t * 2 * D + g * gw
                    qkv[:, c0:c0 + gw] = mm(xn[:DTILE, :], wqkv[:, c0:c0 + gw]).astype(BF)

            def scores(g):
                for b in range(n_pairs):
                    rr = slice(b * pair, (b + 1) * pair)
                    for hh in range(GROUP):
                        c0 = g * gw + hh * HD
                        sc = qk(qkv[rr, c0:c0 + HD], qkv[rr, 2 * D + c0:2 * D + c0 + HD])
                        s_scr[(g % 2) * 16 + b * GROUP + hh, :, :pair] = jnp.where(causal, sc, -1e30)

            def values(g):
                for b in range(n_pairs):
                    rr = slice(b * pair, (b + 1) * pair)
                    for hh in range(GROUP):
                        c0 = g * gw + hh * HD
                        p = p_scr[(g % 2) * 16 + b * GROUP + hh, :, :pair]
                        o[rr, c0:c0 + HD] = mm(p, qkv[rr, 4 * D + c0:4 * D + c0 + HD]).astype(BF)

            def probs(g):
                for j in range(n_pairs * GROUP):
                    j = (g % 2) * 16 + j
                    p_scr[j, :, :pair] = softmax(s_scr[j, :, :pair])

            for g in range(n_groups + 1):
                if g < n_groups:
                    project(g)
                    scores(g)
                    probs(g)
                if g > 0:
                    values(g - 1)
            for n in range(0, D, 512):
                z[r, n:n + 512] = (z[r, n:n + 512].astype(F32) + mm(o[...], wo[:, n:n + 512])).astype(BF)
            return c
        lax.fori_loop(0, tokens // DTILE, self_tile, 0)
        prefetch(layer, 0)
        prefetch(layer, 1)

        w_copy(layer, 2).wait()
        w_copy(layer, 3).wait()
        w_copy(layer, 4).wait()
        for hf in range(2):
            nt = nts[hf]
            h_hbm = (h1_hbm, h2_hbm)[hf]

            def h_copy(i):
                src = h_hbm.at[pl.ds(pl.multiple_of(i * TILE, TILE), TILE), :]
                return pltpu.make_async_copy(src, ht.at[lax.rem(i, 2)], sem_h.at[lax.rem(i, 2)])
            h_copy(0).start()
            kv[pl.ds(pl.multiple_of(nt * TILE, TILE), S_ENC), :] = jnp.zeros((S_ENC, 2 * D), BF)

            def kv_tile(i, c):
                @pl.when(i + 1 < nt)
                def _():
                    h_copy(i + 1).start()
                h_copy(i).wait()
                r = pl.ds(pl.multiple_of(i * TILE, TILE), TILE)
                for n in range(0, 2 * D, D):
                    kv[r, n:n + D] = mm(ht[lax.rem(i, 2)], wkv[:, n:n + D]).astype(BF)
                return c
            lax.fori_loop(0, nt, kv_tile, 0)

            def cross_tile(i, c):
                base = hf * n_half
                r = pl.ds(pl.multiple_of(base * S_DEC + i * DTILE, DTILE), DTILE)
                xn[:DTILE, :] = rms(z[r, :])
                n_b = DTILE // S_DEC
                gw = 2 * GROUP * HD

                def project(g):
                    qkv[:, g * gw:(g + 1) * gw] = mm(xn[:DTILE, :], wq[:, g * gw:(g + 1) * gw]).astype(BF)

                def where_of(b):
                    s = base + i * n_b + b
                    return s, pl.ds(pl.multiple_of(starts[s], 16), S_ENC), slice(b * S_DEC, (b + 1) * S_DEC)

                def scores(g):
                    for b in range(n_b):
                        s, kr, rr = where_of(b)
                        keep = lax.broadcasted_iota(jnp.int32, (pair, S_ENC), 1) < len_ref[s]
                        for hh in range(GROUP):
                            c0 = g * gw + 2 * hh * HD
                            k0 = (g * GROUP + hh) * HD
                            q2 = jnp.concatenate([qkv[rr, c0:c0 + HD], qkv[rr, c0 + HD:c0 + 2 * HD]], axis=0)
                            s_scr[g * 16 + b * GROUP + hh] = jnp.where(keep, qk(q2, kv[kr, k0:k0 + HD]), -1e30)

                def probs(g):
                    for j in range(16):
                        p_scr[g * 16 + j] = softmax(s_scr[g * 16 + j])

                def values(g):
                    for b in range(n_b):
                        s, kr, rr = where_of(b)
                        for hh in range(GROUP):
                            c0 = g * gw + 2 * hh * HD
                            k0 = D + (g * GROUP + hh) * HD
                            res = mm(p_scr[g * 16 + b * GROUP + hh], kv[kr, k0:k0 + HD]).astype(BF)
                            o[rr, c0:c0 + HD] = res[:S_DEC]
                            o[rr, c0 + HD:c0 + 2 * HD] = res[S_DEC:]

                project(0)
                scores(0)
                probs(0)
                project(1)
                scores(1)
                probs(1)
                values(0)
                values(1)
                for n in range(0, D, 512):
                    z[r, n:n + 512] = (z[r, n:n + 512].astype(F32) + mm(o[...], woc[:, n:n + 512])).astype(BF)
                return c
            lax.fori_loop(0, n_half * S_DEC // DTILE, cross_tile, 0)
        prefetch(layer, 2)
        prefetch(layer, 3)
        prefetch(layer, 4)

        w_copy(layer, 5).wait()
        w_copy(layer, 6).wait()

        def ffn_tile(i, c):
            r = pl.ds(pl.multiple_of(i * TILE, TILE), TILE)
            xn[...] = rms(z[r, :])
            for n in range(0, FF, 512):
                hid[:, n:n + 512] = gelu(mm(xn[...], w1[:, n:n + 512])).astype(BF)
            for n in range(0, D, 512):
                z[r, n:n + 512] = (z[r, n:n + 512].astype(F32) + mm(hid[...], w2[:, n:n + 512])).astype(BF)
            return c
        lax.fori_loop(0, tokens // TILE, ffn_tile, 0)
        prefetch(layer, 5)
        prefetch(layer, 6)
        return carry
    lax.fori_loop(0, 2, layer_step, 0)
    out_copy = pltpu.make_async_copy(z, out_hbm, sem_y)
    out_copy.start()
    out_copy.wait()


def decode(lens, y, h1, h2, wqkv, wo, wq, wkv, woc, w1, w2):
    n_seq = lens.shape[0]
    tokens = n_seq * S_DEC
    pad = n_seq // 2 * S_ENC + S_ENC
    cost = pl.CostEstimate(flops=150_000_000_000, bytes_accessed=100_000_000, transcendentals=0)
    return pl.pallas_call(
        lambda *refs: dec_kernel(n_seq, *refs),
        out_shape=jax.ShapeDtypeStruct((tokens, D), BF),
        in_specs=[SMEM] + [ANY] * 10,
        out_specs=ANY,
        scratch_shapes=[
            pltpu.SMEM((n_seq,), jnp.int32),
            pltpu.VMEM((tokens, D), BF),
            pltpu.VMEM((pad, 2 * D), BF),
            pltpu.VMEM((2, TILE, D), BF),
            pltpu.VMEM((DTILE, 6 * D), BF),
            pltpu.VMEM((DTILE, 2 * D), BF),
            pltpu.VMEM((32, 2 * S_DEC, S_ENC), F32),
            pltpu.VMEM((32, 2 * S_DEC, S_ENC), BF),
            pltpu.VMEM((TILE, D), BF),
            pltpu.VMEM((TILE, FF), BF),
            pltpu.VMEM((D, 6 * D), BF),
            pltpu.VMEM((2 * D, D), BF),
            pltpu.VMEM((D, 2 * D), BF),
            pltpu.VMEM((D, 2 * D), BF),
            pltpu.VMEM((2 * D, D), BF),
            pltpu.VMEM((D, FF), BF),
            pltpu.VMEM((FF, D), BF),
            pltpu.SemaphoreType.DMA,
            pltpu.SemaphoreType.DMA((84,)),
            pltpu.SemaphoreType.DMA((2,)),
        ],
        compiler_params=pltpu.CompilerParams(vmem_limit_bytes=VMEM_LIMIT),
        cost_estimate=cost,
        name="decode",
    )(lens, y, h1, h2, wqkv, wo, wq, wkv, woc, w1, w2)


def by_head(w):
    return w.reshape(w.shape[0], D, -1, HD).transpose(0, 2, 1, 3)


def solution(mesh):
    stages = mesh.shape["stage"]
    swap = [(source, (source + stages // 2) % stages) for source in range(stages)]
    rows = P(("data", "stage"))
    whole = P()

    def body(x_enc, enc_len, y, enc_wqkv, enc_wo, enc_w1, enc_w2, dec_wqkv, dec_wo, cross_wq, cross_wkv, cross_wo, dec_w1, dec_w2):
        n_seq = x_enc.shape[0]
        n_half = n_seq // 2
        layers = enc_wqkv.shape[0]
        x_recv = lax.ppermute(x_enc[n_half:].reshape(n_half * S_ENC, D), "stage", swap)
        len_recv = lax.ppermute(enc_len, "stage", swap)
        e_w = (by_head(enc_wqkv), enc_wo.reshape(layers, 2 * D, D), enc_w1, enc_w2)
        h_own = encode(enc_len[:n_half], x_enc.reshape(n_seq * S_ENC, D), *e_w)
        h_first = lax.ppermute(h_own, "stage", swap)
        h_second = encode(len_recv[n_half:], x_recv, *e_w)
        out = decode(
            len_recv, y.reshape(n_seq * S_DEC, D), h_first, h_second,
            by_head(dec_wqkv), dec_wo.reshape(layers, 2 * D, D),
            by_head(cross_wq), by_head(cross_wkv), cross_wo.reshape(layers, 2 * D, D),
            dec_w1, dec_w2)
        return out.reshape(n_seq, S_DEC, D)

    return jax.shard_map(body, mesh=mesh, in_specs=(rows, rows, rows) + (whole,) * 11, out_specs=rows, check_vma=False)
```

time: 1570 us -> 622 us (0.40)
  the two profiles are of different devices: /device:TPU:0 before, /device:TPU:7 now
where the time goes in v1:
time: 622 us; the launch traced here: 612 us
  Pallas kernels  527 us (85%)
  local copies, waits for them, and re-layouts  67.8 us (11%)
  starting transfers between devices  17.4 us (3%)
    pallas_call x2, Pallas kernels, encode(): pl.pallas_call(lambda *refs: enc_kernel(n_seq, *refs), out_shape=jax.Shap...  300 us
    pallas_call x1, Pallas kernels, decode(): pl.pallas_call(lambda *refs: dec_kernel(n_seq, *refs), out_shape=jax.Shap...  226 us
    unnamed x6, local copies, waits for them, and re-layouts  62.4 us
    ppermute x1, starting transfers between devices, body(): h_first = lax.ppermute(h_own, 'stage', swap)  16 us
  transfers between devices with their start and end apart: 3, of which 0 were waited for; matrix products, arithmetic and copies ran while one was open for 11% of the time, Pallas kernels for 49%

profile of v1, /device:TPU:7, one launch (start us, length us, event | category | flops | bytes accessed | tf_op | source)
XLA Modules:
  0.0 612.2 jit_solution(1111393030276058471)
XLA Ops:
  0.0 0.3 collective-permute-start
  0.3 4.8 slice.11
  5.0 1.2 collective-permute-start.2
  6.2 22.5 %copy.15 = bf16[2,1024,3,16,128]{4,1,3,2,0:T(8,128)(2,1)} copy(bf16[2,1024,3,16,128]{4,3,2,1,0:T(8,128)(2,1)} %param.17) | data formatting | bytes 50331648 | tf_op args[3]
  28.7 155.8 %encode.2 = bf16[2048,1024]{1,0:T(8,128)(2,1)} custom-call(s32[16]{0:T(128)} %bitcast.31, bf16[4096,1024]{1,0:T(8,128)(2,1)} %bitcast.25, bf16[2,48,1024,128]{3,2,1,0:T(8,128)(2,1)} %bitcast.21, bf16[2,2048,1024]{2,1,0:T(8,128)(2,1)} %bitcast.26, bf16[2,1024,3072]{2,1,0:T(8,128)(2,1)} %refs_4_.3, bf16[2,3072,1024]{2,1,0:T(8,128)(2,1)} %refs_5_.3), custom_call_target="tpu_custom_call" | custom-call | flops 77824000000 | bytes 70000000 | tf_op jit(solution)/shard_map/encode/pallas_call | solution.py:236
  184.5 16.0 %collective-permute-start.1 = (bf16[2048,1024]{1,0:T(8,128)(2,1)}, bf16[2048,1024]{1,0:T(8,128)(2,1)}, u32[]{:S(2)}, u32[]{:S(2)}) collective-permute-start(bf16[2048,1024]{1,0:T(8,128)(2,1)} %encode.2), channel_id=1, source_target_pairs={{0,2},{1,3},{2,0},{3,1},{4,6},{5,7},{6,4},{7,5}} | collective-permute-start | bytes 12582920 | tf_op jit(solution)/shard_map/ppermute | solution.py:521
  200.5 8.8 %copy.17 = bf16[2,1024,8,2,128]{4,1,3,2,0:T(8,128)(2,1)} copy(bf16[2,1024,8,2,128]{4,3,2,1,0:T(2,128)(2,1)} %param.23) | data formatting | bytes 16777216 | tf_op args[9]
  209.2 8.8 %copy.18 = bf16[2,1024,2,8,128]{4,1,3,2,0:T(8,128)(2,1)} copy(bf16[2,1024,2,8,128]{4,3,2,1,0:T(8,128)(2,1)} %param.24) | data formatting | bytes 16777216 | tf_op args[10]
  218.0 22.4 %copy.16 = bf16[2,1024,3,16,128]{4,1,3,2,0:T(8,128)(2,1)} copy(bf16[2,1024,3,16,128]{4,3,2,1,0:T(8,128)(2,1)} %param.21) | data formatting | bytes 50331648 | tf_op args[7]
  240.4 0.0 collective-permute-done.refs_0_
  240.4 0.0 copy-start
  240.4 0.6 slice.10.refs_0_
  241.0 0.0 collective-permute-done.2.refs_1_
  241.0 144.6 %encode.3.refs_3_ = bf16[2048,1024]{1,0:T(8,128)(2,1)} custom-call(s32[16]{0:T(128)} %slice.10.refs_0_, bf16[2048,1024]{1,0:T(8,128)(2,1)} %collective-permute-done.2.refs_1_, bf16[2,48,1024,128]{3,2,1,0:T(8,128)(2,1)} %bitcast.22, bf16[2,2048,1024]{2,1,0:T(8,128)(2,1)} %bitcast.27, bf16[2,1024,3072]{2,1,0:T(8,128)(2,1)} %refs_4_.3, ...), custom_call_target="tpu_custom_call" | custom-call | flops 77824000000 | bytes 70000000 | tf_op jit(solution)/shard_map/encode/pallas_call | solution.py:236
  385.7 0.0 copy-done
  385.7 0.0 collective-permute-done.1.refs_2_
  385.7 226.1 %decode.1 = bf16[1536,1024]{1,0:T(8,128)(2,1)} custom-call(s32[32]{0:T(128)} %copy-done, bf16[1536,1024]{1,0:T(8,128)(2,1)} %bitcast.30, bf16[2048,1024]{1,0:T(8,128)(2,1)} %collective-permute-done.1.refs_2_, bf16[2048,1024]{1,0:T(8,128)(2,1)} %encode.3.refs_3_, bf16[2,48,1024,128]{3,2,1,0:T(8,128)(2,1)} %bitcast.20, bf16[2,2048,1024]{2,1,0:T(8,128)(2,1)} %bitcast.28, ...), custom_call_target="tpu_custom_call" | custom-call | flops 149999992832 | bytes 100000000 | tf_op jit(solution)/shard_map/decode/pallas_call | solution.py:470
Async XLA Ops:
  0.0 240.4 %collective-permute-start = (s32[32]{0:T(128)}, s32[32]{0:T(128)S(1)}, u32[]{:S(2)}, u32[]{:S(2)}) collective-permute-start(s32[32]{0:T(128)} %param.15), channel_id=1, source_target_pairs={{0,2},{1,3},{2,0},{3,1},{4,6},{5,7},{6,4},{7,5}} | collective-permute-start | bytes 392 | tf_op jit(solution)/shard_map/ppermute | solution.py:518
  5.0 236.0 %collective-permute-start.2 = (bf16[2048,1024]{1,0:T(8,128)(2,1)}, bf16[2048,1024]{1,0:T(8,128)(2,1)}, u32[]{:S(2)}, u32[]{:S(2)}) collective-permute-start(bf16[2048,1024]{1,0:T(8,128)(2,1)} %bitcast.5), channel_id=1, source_target_pairs={{0,2},{1,3},{2,0},{3,1},{4,6},{5,7},{6,4},{7,5}} | collective-permute-start | bytes 12582920 | tf_op jit(solution)/shard_map/ppermute | solution.py:517
  184.5 201.2 %collective-permute-start.1 = (bf16[2048,1024]{1,0:T(8,128)(2,1)}, bf16[2048,1024]{1,0:T(8,128)(2,1)}, u32[]{:S(2)}, u32[]{:S(2)}) collective-permute-start(bf16[2048,1024]{1,0:T(8,128)(2,1)} %encode.2), channel_id=1, source_target_pairs={{0,2},{1,3},{2,0},{3,1},{4,6},{5,7},{6,4},{7,5}} | collective-permute-start | bytes 12582920 | tf_op jit(solution)/shard_map/ppermute | solution.py:521
  240.4 145.2 %copy-start = (s32[32]{0:T(128)}, s32[32]{0:T(128)S(1)}, u32[]{:S(2)}) copy-start(s32[32]{0:T(128)S(1)} %collective-permute-done.refs_0_) | copy-start | bytes 388
